TPU v7x, 256 devices: a whole 4x4x8 slice. The times are simulated.
256 devices in a mesh: seq: 2 (over core), ctx: 32 (over x, z_hi, y), tp: 4 (over z_lo).
Axes of the slice: x: 4, y: 4, z: 8 (z_hi: 2, z_lo: 4; z = z_hi * 4 + z_lo), core: 2. Of those that a mesh axis runs over, the one named last changes fastest.
Arguments:
- queries: bfloat16 [16384, 16, 128], P(('seq', 'ctx'), 'tp'), parts along dimension 0, may hold values from -160 to 160
- key_rows: bfloat16 [16384, 4, 128], P(('seq', 'ctx'), 'tp'), parts along dimension 0, may hold values from -5 to 5
- value_slot_rows: bfloat16 [16384, 4, 128], P(('seq', 'ctx'), 'tp'), parts along dimension 0, may hold values from -6 to 6
- out_grad: bfloat16 [16384, 16, 128], P(('seq', 'ctx'), 'tp'), parts along dimension 0, may hold values from -6 to 6
- span_order: int32 [128], P('seq'), parts along dimension 0, may hold values from 0 to 63, each once
Outputs:
- query_grad: bfloat16 [16384, 16, 128], P(('seq', 'ctx'), 'tp'), parts along dimension 0
- key_gradient: bfloat16 [16384, 4, 128], P(('seq', 'ctx'), 'tp'), parts along dimension 0
- value_gradient: bfloat16 [16384, 4, 128], P(('seq', 'ctx'), 'tp'), parts along dimension 0
There are 2 independent parts, one for each index of `seq`. A program takes and returns all parts, laid end to end along the dimension named above; each array names one. Nothing has to cross between parts.
Inputs may be any that keep to these rules, and one draw needn't show every extreme that they name: Slot s of 128 rows holds span span_order[s] of the sequence; every span number stands once.
All inputs are finite; a program needn't handle non-finite values.
Results may differ from a plain program's by a relative error of at most 0.0085.
Values may be sent and summed in bfloat16 or wider, within the bound.
No kernel may reach another device: no remote copies, remote signals or barrier semaphores. Data moves between devices by JAX's collectives and lax.ppermute only.
A program may use at most 64 MiB of HBM per device.

v0:
```python
import math

import jax
import jax.numpy as jnp
from jax import lax
from jax.experimental import pallas as pl
from jax.experimental.pallas import tpu as pltpu
from jax.sharding import PartitionSpec as P


NEG = -1e30
X, Z, Y = 4, 2, 4
SPAN = 128
D = 128
HEADS = 4
ROWS = HEADS * SPAN
LOCAL = 2
LINE = (0, 1, 3, 2)
NEAR = LINE[:-1]
PLANE = tuple((w, t) for w in range(Z) for t in range(Y))
HALF = Y * LOCAL
SCALE = 1.0 / math.sqrt(D)
C2 = SCALE * math.log2(math.e)
UNROLL = 2
COST = 1
FAR = 60.0


def ctx_index(x, z, y):
    return (x * Z + z) * Y + y


def shift(dx=0, dz=0, dy=0):
    return [
        (ctx_index((x + dx) % X, (z + dz) % Z, (y + dy) % Y), ctx_index(x, z, y))
        for x in range(X)
        for z in range(Z)
        for y in range(Y)
    ]


def fetch(a, **d):
    return lax.ppermute(a, "ctx", shift(**d))


def plan(rows, keys, group, order_ref, pos_ref, rank_ref, kspan_ref, rspan_ref):
    x, z, y = pos_ref[0], pos_ref[1], pos_ref[2]
    for i, s in enumerate(rows):
        dev = ((x + s) % X * Z + z) * Y + y
        for e in range(LOCAL):
            rspan_ref[i * LOCAL + e] = order_ref[dev * LOCAL + e]
    ks = []
    for w, t in keys:
        dev = (x * Z + (z + w) % Z) * Y + (y + t) % Y
        for e in range(LOCAL):
            k = order_ref[dev * LOCAL + e]
            kspan_ref[len(ks)] = k
            ks.append(k)
    for i in range(len(ks)):
        base = i // group * group
        r = jnp.int32(base)
        for j in range(base, base + group):
            if j != i:
                r = r + (ks[j] < ks[i]).astype(jnp.int32)
        rank_ref[r] = i


def pairs_upto(kspan_ref, base, n, p):
    upto = jnp.int32(1)
    for i in range(n):
        upto = upto + (kspan_ref[base + i] <= p).astype(jnp.int32)
    return upto // 2


def take(qg, kv, qs, gs, ks, vs):
    spans = [(ref, e) for ref in qg for e in range(ref.shape[0])]
    for i, (ref, e) in enumerate(spans):
        qs[i] = ref[e, 0]
        gs[i] = ref[e, 1]
    for i, ref in enumerate(kv):
        for e in range(LOCAL):
            ks[i * LOCAL + e] = ref[0, e]
            vs[i * LOCAL + e] = ref[1, e]


def pair_of(ref, a, b):
    return jnp.concatenate([ref[a], ref[b]], axis=0)


def nt(a, b):
    return lax.dot_general(a, b, (((1,), (1,)), ((), ())), preferred_element_type=jnp.float32)


def nn(a, b):
    return lax.dot_general(a, b, (((1,), (0,)), ((), ())), preferred_element_type=jnp.float32)


def hide(st, kspan_ref, a, b, p):
    key = lax.broadcasted_iota(jnp.int32, (SPAN, ROWS), 0)
    row = lax.broadcasted_iota(jnp.int32, (SPAN, ROWS), 1) % SPAN
    ahead = key - row
    sa = jnp.where(ahead <= (p - kspan_ref[a]) * SPAN, st[:SPAN], NEG)
    sb = jnp.where(ahead <= (p - kspan_ref[b]) * SPAN, st[SPAN:], NEG)
    return jnp.concatenate([sa, sb], axis=0)


def below(x):
    return jnp.sum(x, axis=0, keepdims=True)


def stats_kernel(rows, keys, order_ref, pos_ref, *refs):
    nq, nk = len(rows), len(keys)
    first = nk == Y
    n = nq if first else nq + 1
    qg = refs[:n]
    kv = refs[n : n + nk]
    refs = refs[n + nk :]
    if not first:
        init_ref, refs = refs[0], refs[1:]
    out_ref, qs, gs, ks, vs, over_ref, rank_ref, kspan_ref, rspan_ref = refs
    plan(rows, keys, HALF, order_ref, pos_ref, rank_ref, kspan_ref, rspan_ref)
    take(qg, kv, qs, gs, ks, vs)
    over_ref[...] = jnp.zeros_like(over_ref)

    def begin():
        for i in range(nq):
            if not first and i < len(NEAR):
                out_ref[i] = init_ref[i]
            else:
                out_ref[i, 0] = jnp.full((LOCAL * HEADS, SPAN), NEG, jnp.float32)
                out_ref[i, 1] = jnp.zeros((LOCAL * HEADS, SPAN), jnp.float32)
                out_ref[i, 2] = jnp.zeros((LOCAL * HEADS, SPAN), jnp.float32)

    if first:
        jobs = nq * LOCAL
    else:
        jobs = (nq - len(NEAR)) * LOCAL + nq * LOCAL

    def work(job, careful):
        if first:
            r, base = job, 0
        else:
            early = job < jobs - nq * LOCAL
            r = jnp.where(early, job + len(NEAR) * LOCAL, job - (jobs - nq * LOCAL))
            base = jnp.where(early, 0, HALF)
        p = rspan_ref[r]
        pairs = pairs_upto(kspan_ref, base, HALF, p)

        def get():
            return tuple(
                jnp.concatenate(
                    [out_ref[r // 2, i, pl.ds(r % 2 * HEADS + h, 1), :] for h in range(HEADS)], axis=1
                )
                for i in range(3)
            )

        def put(carried):
            for i in range(3):
                for h in range(HEADS):
                    out_ref[r // 2, i, pl.ds(r % 2 * HEADS + h, 1), :] = carried[i][:, h * SPAN : (h + 1) * SPAN]

        def products(j):
            a, b = rank_ref[base + 2 * j], rank_ref[base + 2 * j + 1]
            return nt(pair_of(ks, a, b), qs[r]), nt(pair_of(vs, a, b), gs[r]), a, b

        def exact(j, carried):
            m, l, d = carried
            st, dp, a, b = products(j)
            st = hide(st, kspan_ref, a, b, p)
            top = jnp.maximum(m, jnp.max(st, axis=0, keepdims=True))
            keep = jnp.exp2((m - top) * C2)
            e = jnp.exp2((st - top) * C2)
            return top, l * keep + below(e), d * keep + below(e * dp)

        def quick(j, n, ref, carried):
            m, l, d = carried
            for i in range(n):
                st, dp, _, _ = products(j + i)
                m = jnp.maximum(m, jnp.max(st, axis=0, keepdims=True))
                e = jnp.exp2(st * C2 - ref)
                l = l + below(e)
                d = d + below(e * dp)
            return m, l, d

        if careful:
            put(lax.fori_loop(0, pairs, exact, get()))
            return

        @pl.when(pairs > 0)
        def _():
            m, l, d = exact(pairs - 1, get())
            rest = pairs - 1
            many = rest // UNROLL
            ref = m * C2
            state = lax.fori_loop(0, many, lambda j, c: quick(j * UNROLL, UNROLL, ref, c), (m, l, d))
            top, l, d = lax.fori_loop(many * UNROLL, rest, lambda j, c: quick(j, 1, ref, c), state)
            put((m, l, d))
            over_ref[...] = jnp.maximum(over_ref[...], top - m)

    begin()

    @pl.loop(0, jobs)
    def _(job):
        work(job, False)

    @pl.when(jnp.max(over_ref[...]) * C2 > FAR)
    def _():
        begin()

        @pl.loop(0, jobs)
        def _(job):
            work(job, True)


def grads_kernel(order_ref, pos_ref, *refs):
    qg = refs[: X + 1]
    kv = refs[X + 1 : X + 1 + Y * Z]
    n = X + 1 + Y * Z
    st_refs = refs[n : n + X]
    n = n + X
    dq_refs = refs[n : n + X]
    dkv_refs = refs[n + X : n + X + Y * Z]
    qs, gs, ks, vs, kt, lse_ref, delta_ref, dqt, dk, dv, rank_ref, kspan_ref, rspan_ref = refs[n + X + Y * Z :]
    nk = Y * Z * LOCAL
    plan(LINE, PLANE, nk, order_ref, pos_ref, rank_ref, kspan_ref, rspan_ref)
    take(qg, kv, qs, gs, ks, vs)
    for i in range(nk):
        kt[i] = ks[i].T
    for i, s in enumerate(LINE):
        parts = [st_refs[t][LINE.index((s - t) % X)] for t in range(X)]
        top = parts[0][0]
        for q in parts[1:]:
            top = jnp.maximum(top, q[0])
        total = jnp.zeros_like(top)
        dots = jnp.zeros_like(top)
        for q in parts:
            f = jnp.exp2((q[0] - top) * C2)
            total = total + q[1] * f
            dots = dots + q[2] * f
        lse_ref[pl.ds(i * 8, 8), :] = top * C2 + jnp.log2(total)
        delta_ref[pl.ds(i * 8, 8), :] = dots / total
    dk[...] = jnp.zeros_like(dk)
    dv[...] = jnp.zeros_like(dv)

    @pl.loop(0, X * LOCAL)
    def _(r):
        p = rspan_ref[r]
        pairs = pairs_upto(kspan_ref, 0, nk, p)
        lse = jnp.concatenate([lse_ref[pl.ds(r * HEADS + h, 1), :] for h in range(HEADS)], axis=1)
        delta = jnp.concatenate([delta_ref[pl.ds(r * HEADS + h, 1), :] for h in range(HEADS)], axis=1)

        def tile(j, n, masked):
            q, g = qs[r], gs[r]
            to_q = None
            for i in range(n):
                a, b = rank_ref[2 * (j + i)], rank_ref[2 * (j + i) + 1]
                st = nt(pair_of(ks, a, b), q)
                dp = nt(pair_of(vs, a, b), g)
                if masked:
                    st = hide(st, kspan_ref, a, b, p)
                pt = jnp.exp2(st * C2 - lse)
                ds = (pt * (dp - delta)).astype(jnp.bfloat16)
                dvt = nn(pt.astype(jnp.bfloat16), g)
                dkt = nn(ds, q)
                dv[a] += dvt[:SPAN]
                dv[b] += dvt[SPAN:]
                dk[a] += dkt[:SPAN]
                dk[b] += dkt[SPAN:]
                part = nn(jnp.concatenate([kt[a], kt[b]], axis=1), ds)
                to_q = part if to_q is None else to_q + part
            if masked:
                dqt[r] = to_q
            else:
                dqt[r] += to_q

        @pl.when(pairs == 0)
        def _():
            dqt[r] = jnp.zeros((D, ROWS), jnp.float32)

        @pl.when(pairs > 0)
        def _():
            tile(pairs - 1, 1, True)
            many = (pairs - 1) // UNROLL

            @pl.loop(0, many)
            def _(j):
                tile(j * UNROLL, UNROLL, False)

            @pl.loop(many * UNROLL, pairs - 1)
            def _(j):
                tile(j, 1, False)

    for i in range(X):
        for e in range(LOCAL):
            dq_refs[i][e] = (dqt[i * LOCAL + e] * SCALE).T.astype(jnp.bfloat16)
    for i in range(Y * Z):
        for e in range(LOCAL):
            dkv_refs[i][0, e] = (dk[i * LOCAL + e] * SCALE).astype(jnp.bfloat16)
            dkv_refs[i][1, e] = dv[i * LOCAL + e].astype(jnp.bfloat16)


SMEM = pl.BlockSpec(memory_space=pltpu.SMEM)
VMEM = pl.BlockSpec(memory_space=pltpu.VMEM)


def index_scratch(nq, nk):
    return [
        pltpu.SMEM((nk * LOCAL,), jnp.int32),
        pltpu.SMEM((nk * LOCAL,), jnp.int32),
        pltpu.SMEM((nq * LOCAL,), jnp.int32),
    ]


def operand_scratch(nq, nk):
    return [
        pltpu.VMEM((nq * LOCAL, ROWS, D), jnp.bfloat16),
        pltpu.VMEM((nq * LOCAL, ROWS, D), jnp.bfloat16),
        pltpu.VMEM((nk * LOCAL, SPAN, D), jnp.bfloat16),
        pltpu.VMEM((nk * LOCAL, SPAN, D), jnp.bfloat16),
    ]


def cost(nq, nk, products):
    return pl.CostEstimate(
        flops=nq * nk * LOCAL * ROWS * LOCAL * SPAN * D * 2 * products * COST,
        bytes_accessed=(nq * 4 * ROWS + nk * 4 * SPAN) * D * 2,
        transcendentals=0,
    )


def stats_call(order, pos, qg, kv, rows, keys, *init):
    nq, nk = len(rows), len(keys)
    return pl.pallas_call(
        lambda *refs: stats_kernel(rows, keys, *refs),
        out_shape=jax.ShapeDtypeStruct((nq, 3, LOCAL * HEADS, SPAN), jnp.float32),
        in_specs=[SMEM, SMEM] + [VMEM] * (len(qg) + nk + len(init)),
        out_specs=VMEM,
        scratch_shapes=operand_scratch(nq, nk) + [pltpu.VMEM((1, ROWS), jnp.float32)] + index_scratch(nq, nk),
        compiler_params=pltpu.CompilerParams(vmem_limit_bytes=48 * 2**20),
        cost_estimate=cost(nq, nk, 2),
        name="row_stats",
    )(order, pos, *qg, *kv, *init)


def grads_call(order, pos, qg, kv, stats):
    nk = Y * Z * LOCAL
    return pl.pallas_call(
        grads_kernel,
        out_shape=[jax.ShapeDtypeStruct((LOCAL, ROWS, D), jnp.bfloat16)] * X
        + [jax.ShapeDtypeStruct((2, LOCAL, SPAN, D), jnp.bfloat16)] * (Y * Z),
        in_specs=[SMEM, SMEM] + [VMEM] * (len(qg) + len(kv) + len(stats)),
        out_specs=[VMEM] * (X + Y * Z),
        scratch_shapes=operand_scratch(X, Y * Z)
        + [
            pltpu.VMEM((nk, D, SPAN), jnp.bfloat16),
            pltpu.VMEM((X * LOCAL * HEADS, SPAN), jnp.float32),
            pltpu.VMEM((X * LOCAL * HEADS, SPAN), jnp.float32),
            pltpu.VMEM((X * LOCAL, D, ROWS), jnp.float32),
            pltpu.VMEM((nk, SPAN, D), jnp.float32),
            pltpu.VMEM((nk, SPAN, D), jnp.float32),
        ]
        + index_scratch(X, Y * Z),
        compiler_params=pltpu.CompilerParams(vmem_limit_bytes=48 * 2**20),
        cost_estimate=cost(X, Y * Z, 5),
        name="gradients",
    )(order, pos, *qg, *kv, *stats)


def by_head(a):
    return a.reshape(LOCAL, SPAN, HEADS, D).transpose(0, 2, 1, 3).reshape(LOCAL, ROWS, D)


def step(queries, key_rows, value_slot_rows, out_grad, span_order):
    me = lax.axis_index("ctx")
    pos = jnp.stack([me // (Z * Y), me // Y % Z, me % Y]).astype(jnp.int32)
    kv0 = jnp.stack([key_rows.reshape(LOCAL, SPAN, D), value_slot_rows.reshape(LOCAL, SPAN, D)])
    qg0 = jnp.stack([by_head(queries), by_head(out_grad)], axis=1)
    kvz = fetch(kv0, dz=1)
    qg = [qg0, fetch(qg0, dx=1), fetch(qg0, dx=3)]
    kv = [kv0] + [fetch(kv0, dy=t) for t in range(1, Y)]
    part = stats_call(span_order, pos, qg, kv, NEAR, PLANE[:Y])
    qg += [fetch(qg[1][:1], dx=1), fetch(qg[2][1:], dx=3)]
    kv += [kvz] + [fetch(kvz, dy=t) for t in range(1, Y)]
    stats0 = stats_call(span_order, pos, qg, kv, LINE, PLANE, part)
    stats = [stats0] + [fetch(stats0, dx=t) for t in range(1, X)]
    out = grads_call(span_order, pos, qg, kv, stats)
    dq, own, other = out[:X], out[X : X + Y], out[X + Y :]

    def add(parts):
        total = parts[0].astype(jnp.float32)
        for p in parts[1:]:
            total = total + p.astype(jnp.float32)
        return total

    other = add([other[0]] + [fetch(other[t], dy=-t) for t in range(1, Y)]).astype(jnp.bfloat16)
    other = fetch(other, dz=1)
    own = add([own[0]] + [fetch(own[t], dy=-t) for t in range(1, Y)] + [other]).astype(jnp.bfloat16)
    key_gradient = own[0].reshape(LOCAL * SPAN, 1, D)
    value_gradient = own[1].reshape(LOCAL * SPAN, 1, D)
    total = add([dq[0]] + [fetch(dq[i], dx=-s) for i, s in enumerate(LINE) if i > 0])
    query_grad = (
        total.astype(jnp.bfloat16)
        .reshape(LOCAL, HEADS, SPAN, D)
        .transpose(0, 2, 1, 3)
        .reshape(LOCAL * SPAN, HEADS, D)
    )
    return query_grad, key_gradient, value_gradient


def solution(mesh):
    spec = P(("seq", "ctx"), "tp", None)
    return jax.shard_map(
        step,
        mesh=mesh,
        in_specs=(spec, spec, spec, spec, P("seq")),
        out_specs=(spec, spec, spec),
        check_vma=False,
    )
```

profile of v0, /device:TPU:2, one launch (start us, length us, event | category | flops | bytes accessed | tf_op | source)
XLA Modules:
  0.0 104.0 jit_solution(8192751265451658744)
XLA Ops:
  0.6 0.0 copy-start.1
  0.6 1.0 copy.8
  1.7 0.0 copy-done.1
  1.7 0.0 copy-start.2
  1.7 0.0 copy-start.3
  1.8 0.1 pad_maximum_fusion.refs_2_.refs_0_
  1.8 1.6 %collective-permute-start.1 = (bf16[2,2,512,128]{3,2,1,0:T(8,128)(2,1)S(1)}, bf16[2,2,512,128]{3,2,1,0:T(8,128)(2,1)S(1)}, u32[]{:S(2)}, u32[]{:S(2)}) collective-permute-start(bf16[2,2,512,128]{3,2,1,0:T(8,128)(2,1)S(1)} %pad_maximum_fusion.refs_2_.refs_0_), channel_id=1, source_target_pairs={{96,0},{100,4},{104,8},{108,12},{112,16},{116,20},{120,24},{124,28... | collective-permute-start | bytes 1572872 | tf_op jit(solution)/shard_map/ppermute | solution.py:43
  3.4 0.8 collective-permute-start
  4.2 0.0 copy-done.2
  4.2 7.0 %collective-permute-start.7 = (bf16[2,2,128,128]{3,2,1,0:T(8,128)(2,1)S(1)}, bf16[2,2,128,128]{3,2,1,0:T(8,128)(2,1)S(1)}, u32[]{:S(2)}, u32[]{:S(2)}) collective-permute-start(bf16[2,2,128,128]{3,2,1,0:T(8,128)(2,1)S(1)} %pad_maximum_fusion.1.refs_5_.refs_7_), channel_id=1, source_target_pairs={{16,0},{20,4},{24,8},{28,12},{0,16},{4,20},{8,24},{12,28},{48,32},... | collective-permute-start | bytes 393224 | tf_op jit(solution)/shard_map/ppermute | solution.py:43
  11.2 1.6 %collective-permute-start.6 = (bf16[2,2,128,128]{3,2,1,0:T(8,128)(2,1)S(1)}, bf16[2,2,128,128]{3,2,1,0:T(8,128)(2,1)S(1)}, u32[]{:S(2)}, u32[]{:S(2)}) collective-permute-start(bf16[2,2,128,128]{3,2,1,0:T(8,128)(2,1)S(1)} %pad_maximum_fusion.1.refs_5_.refs_7_), channel_id=1, source_target_pairs={{12,0},{0,4},{4,8},{8,12},{28,16},{16,20},{20,24},{24,28},{44,32},... | collective-permute-start | bytes 393224 | tf_op jit(solution)/shard_map/ppermute | solution.py:43
  12.8 2.9 %collective-permute-start.5 = (bf16[2,2,128,128]{3,2,1,0:T(8,128)(2,1)S(1)}, bf16[2,2,128,128]{3,2,1,0:T(8,128)(2,1)S(1)}, u32[]{:S(2)}, u32[]{:S(2)}) collective-permute-start(bf16[2,2,128,128]{3,2,1,0:T(8,128)(2,1)S(1)} %pad_maximum_fusion.1.refs_5_.refs_7_), channel_id=1, source_target_pairs={{8,0},{12,4},{0,8},{4,12},{24,16},{28,20},{16,24},{20,28},{40,32},... | collective-permute-start | bytes 393224 | tf_op jit(solution)/shard_map/ppermute | solution.py:43
  15.7 0.0 collective-permute-done.1.refs_4_.refs_2_
  15.7 2.9 %collective-permute-start.4 = (bf16[2,2,128,128]{3,2,1,0:T(8,128)(2,1)S(1)}, bf16[2,2,128,128]{3,2,1,0:T(8,128)(2,1)S(1)}, u32[]{:S(2)}, u32[]{:S(2)}) collective-permute-start(bf16[2,2,128,128]{3,2,1,0:T(8,128)(2,1)S(1)} %pad_maximum_fusion.1.refs_5_.refs_7_), channel_id=1, source_target_pairs={{4,0},{8,4},{12,8},{0,12},{20,16},{24,20},{28,24},{16,28},{36,32},... | collective-permute-start | bytes 393224 | tf_op jit(solution)/shard_map/ppermute | solution.py:43
  18.6 0.0 collective-permute-done.refs_3_.refs_1_
  18.6 1.6 %collective-permute-start.3 = (bf16[1,2,512,128]{3,2,1,0:T(8,128)(2,1)S(1)}, bf16[1,2,512,128]{3,2,1,0:T(8,128)(2,1)S(1)}, u32[]{:S(2)}, u32[]{:S(2)}) collective-permute-start(bf16[1,2,512,128]{3,2,1,0:T(8,128)(2,1)S(1)} %slice.17), channel_id=1, source_target_pairs={{96,0},{100,4},{104,8},{108,12},{112,16},{116,20},{120,24},{124,28... | collective-permute-start | bytes 786440 | tf_op jit(solution)/shard_map/ppermute | solution.py:43
  20.2 0.0 collective-permute-done.7.refs_11_.refs_9_
  20.2 0.6 collective-permute-start.2
  20.8 0.1 pad_add_fusion.refs_1_.pos_ref
  20.9 0.0 collective-permute-done.6.refs_8_.refs_10_
  20.9 0.0 collective-permute-start.10
  20.9 0.0 collective-permute-done.5.refs_7_.refs_9_
  20.9 2.5 %collective-permute-start.9 = (bf16[2,2,128,128]{3,2,1,0:T(8,128)(2,1)S(1)}, bf16[2,2,128,128]{3,2,1,0:T(8,128)(2,1)S(1)}, u32[]{:S(2)}, u32[]{:S(2)}) collective-permute-start(bf16[2,2,128,128]{3,2,1,0:T(8,128)(2,1)S(1)} %collective-permute-done.7.refs_11_.refs_9_), channel_id=1, source_target_pairs={{8,0},{12,4},{0,8},{4,12},{24,16},{28,20},{16,24},{20,28},{40,32},... | collective-permute-start | bytes 393224 | tf_op jit(solution)/shard_map/ppermute | solution.py:43
  23.5 0.0 collective-permute-done.4.refs_6_.refs_8_
  23.5 1.3 %collective-permute-start.8 = (bf16[2,2,128,128]{3,2,1,0:T(8,128)(2,1)S(1)}, bf16[2,2,128,128]{3,2,1,0:T(8,128)(2,1)S(1)}, u32[]{:S(2)}, u32[]{:S(2)}) collective-permute-start(bf16[2,2,128,128]{3,2,1,0:T(8,128)(2,1)S(1)} %collective-permute-done.7.refs_11_.refs_9_), channel_id=1, source_target_pairs={{4,0},{8,4},{12,8},{0,12},{20,16},{24,20},{28,24},{16,28},{36,32},... | collective-permute-start | bytes 393224 | tf_op jit(solution)/shard_map/ppermute | solution.py:43
  24.8 5.8 %row_stats.2.refs_15_ = f32[3,3,8,128]{3,2,1,0:T(8,128)S(1)} custom-call(s32[64]{0:T(128)S(1)} %copy-done, s32[3]{0:T(128)S(1)} %pad_add_fusion.refs_1_.pos_ref, bf16[2,2,512,128]{3,2,1,0:T(8,128)(2,1)S(1)} %pad_maximum_fusion.refs_2_.refs_0_, bf16[2,2,512,128]{3,2,1,0:T(8,128)(2,1)S(1)} %collective-permute-done.refs_3_.refs_1_, ...), custom_call_target="tpu_custom_call" | custom-call | flops 1610612736 | bytes 2097152 | tf_op jit(solution)/shard_map/row_stats/pallas_call | solution.py:333
  30.7 0.0 collective-permute-done.10.refs_14_.refs_12_
  30.7 0.0 collective-permute-done.9.refs_13_.refs_11_
  30.7 0.0 collective-permute-done.8.refs_12_.refs_10_
  30.7 0.0 collective-permute-done.3.refs_6_.refs_4_
  30.7 0.0 collective-permute-done.2.refs_5_.refs_3_
  30.7 6.8 %row_stats.3.refs_13_ = f32[4,3,8,128]{3,2,1,0:T(8,128)S(1)} custom-call(s32[64]{0:T(128)S(1)} %copy-done, s32[3]{0:T(128)S(1)} %pad_add_fusion.refs_1_.pos_ref, bf16[2,2,512,128]{3,2,1,0:T(8,128)(2,1)S(1)} %pad_maximum_fusion.refs_2_.refs_0_, bf16[2,2,512,128]{3,2,1,0:T(8,128)(2,1)S(1)} %collective-permute-done.refs_3_.refs_1_, ...), custom_call_target="tpu_custom_call" | custom-call | flops 4294967296 | bytes 3145728 | tf_op jit(solution)/shard_map/row_stats/pallas_call | solution.py:333
  37.5 10.8 %collective-permute-start.13 = (f32[4,3,8,128]{3,2,1,0:T(8,128)S(1)}, f32[4,3,8,128]{3,2,1,0:T(8,128)S(1)}, u32[]{:S(2)}, u32[]{:S(2)}) collective-permute-start(f32[4,3,8,128]{3,2,1,0:T(8,128)S(1)} %row_stats.3.refs_13_), channel_id=1, source_target_pairs={{96,0},{100,4},{104,8},{108,12},{112,16},{116,20},{120,24},{124,28... | collective-permute-start | bytes 147464 | tf_op jit(solution)/shard_map/ppermute | solution.py:43
  48.4 0.0 collective-permute-start.12
  48.4 2.3 %collective-permute-start.11 = (f32[4,3,8,128]{3,2,1,0:T(8,128)S(1)}, f32[4,3,8,128]{3,2,1,0:T(8,128)S(1)}, u32[]{:S(2)}, u32[]{:S(2)}) collective-permute-start(f32[4,3,8,128]{3,2,1,0:T(8,128)S(1)} %row_stats.3.refs_13_), channel_id=1, source_target_pairs={{32,0},{36,4},{40,8},{44,12},{48,16},{52,20},{56,24},{60,28},{64,3... | collective-permute-start | bytes 147464 | tf_op jit(solution)/shard_map/ppermute | solution.py:43
  50.7 0.0 collective-permute-done.13.refs_16_
  50.7 3.2 %collective-permute-done.12.refs_15_ = f32[4,3,8,128]{3,2,1,0:T(8,128)S(1)} collective-permute-done((f32[4,3,8,128]{3,2,1,0:T(8,128)S(1)}, f32[4,3,8,128]{3,2,1,0:T(8,128)S(1)}, u32[]{:S(2)}, u32[]{:S(2)}) %collective-permute-start.12) | collective-permute-done | bytes 49184 | tf_op jit(solution)/shard_map/ppermute | solution.py:43
  53.9 0.0 collective-permute-done.11.refs_14_
  54.0 16.2 %gradients.1 = (bf16[2,512,128]{2,1,0:T(8,128)(2,1)S(1)}, bf16[2,512,128]{2,1,0:T(8,128)(2,1)S(1)}, bf16[2,512,128]{2,1,0:T(8,128)(2,1)S(1)}, bf16[2,512,128]{2,...) custom-call(s32[64]{0:T(128)S(1)} %copy-done, ...), custom_call_target="tpu_custom_call" | custom-call | flops 10737418240 | bytes 3145728 | tf_op jit(solution)/shard_map/gradients/pallas_call | solution.py:347
  70.2 0.1 collective-permute-start.20
  70.3 1.2 %collective-permute-start.21 = (bf16[2,2,128,128]{3,2,1,0:T(8,128)(2,1)S(1)}, bf16[2,2,128,128]{3,2,1,0:T(8,128)(2,1)S(1)}, u32[]{:S(2)}, u32[]{:S(2)}) collective-permute-start(bf16[2,2,128,128]{3,2,1,0:T(8,128)(2,1)S(1)} %get-tuple-element.25), channel_id=1, source_target_pairs={{8,0},{12,4},{0,8},{4,12},{24,16},{28,20},{16,24},{20,28},{40,32},... | collective-permute-start | bytes 393224 | tf_op jit(solution)/shard_map/ppermute | solution.py:43
  71.5 2.0 %collective-permute-start.22 = (bf16[2,2,128,128]{3,2,1,0:T(8,128)(2,1)S(1)}, bf16[2,2,128,128]{3,2,1,0:T(8,128)(2,1)S(1)}, u32[]{:S(2)}, u32[]{:S(2)}) collective-permute-start(bf16[2,2,128,128]{3,2,1,0:T(8,128)(2,1)S(1)} %get-tuple-element.26), channel_id=1, source_target_pairs={{4,0},{8,4},{12,8},{0,12},{20,16},{24,20},{28,24},{16,28},{36,32},... | collective-permute-start | bytes 393224 | tf_op jit(solution)/shard_map/ppermute | solution.py:43
  73.5 0.9 collective-permute-start.17
  74.4 2.1 %collective-permute-start.18 = (bf16[2,2,128,128]{3,2,1,0:T(8,128)(2,1)S(1)}, bf16[2,2,128,128]{3,2,1,0:T(8,128)(2,1)S(1)}, u32[]{:S(2)}, u32[]{:S(2)}) collective-permute-start(bf16[2,2,128,128]{3,2,1,0:T(8,128)(2,1)S(1)} %get-tuple-element.21), channel_id=1, source_target_pairs={{8,0},{12,4},{0,8},{4,12},{24,16},{28,20},{16,24},{20,28},{40,32},... | collective-permute-start | bytes 393224 | tf_op jit(solution)/shard_map/ppermute | solution.py:43
  76.4 2.4 %collective-permute-done.20 = bf16[2,2,128,128]{3,2,1,0:T(8,128)(2,1)S(1)} collective-permute-done((bf16[2,2,128,128]{3,2,1,0:T(8,128)(2,1)S(1)}, bf16[2,2,128,128]{3,2,1,0:T(8,128)(2,1)S(1)}, u32[]{:S(2)}, u32[]{:S(2)}) %collective-permute-start.20) | collective-permute-done | bytes 131104 | tf_op jit(solution)/shard_map/ppermute | solution.py:43
  78.8 0.2 collective-permute-start.19
  79.1 0.0 collective-permute-done.21
  79.1 0.4 collective-permute-done.22
  79.5 0.1 add_convert_fusion.2
  79.5 11.4 %collective-permute-start.23 = (bf16[2,2,128,128]{3,2,1,0:T(8,128)(2,1)S(1)}, bf16[2,2,128,128]{3,2,1,0:T(8,128)(2,1)S(1)}, u32[]{:S(2)}, u32[]{:S(2)}) collective-permute-start(bf16[2,2,128,128]{3,2,1,0:T(8,128)(2,1)S(1)} %add_convert_fusion.2), channel_id=1, source_target_pairs={{16,0},{20,4},{24,8},{28,12},{0,16},{4,20},{8,24},{12,28},{48,32},... | collective-permute-start | bytes 393224 | tf_op jit(solution)/shard_map/ppermute | solution.py:43
  90.9 2.9 %collective-permute-start.14 = (bf16[2,512,128]{2,1,0:T(8,128)(2,1)S(1)}, bf16[2,512,128]{2,1,0:T(8,128)(2,1)S(1)}, u32[]{:S(2)}, u32[]{:S(2)}) collective-permute-start(bf16[2,512,128]{2,1,0:T(8,128)(2,1)S(1)} %get-tuple-element.16), channel_id=1, source_target_pairs={{96,0},{100,4},{104,8},{108,12},{112,16},{116,20},{120,24},{124,28... | collective-permute-start | bytes 786440 | tf_op jit(solution)/shard_map/ppermute | solution.py:43
  93.8 0.0 collective-permute-done.17
  93.8 0.0 collective-permute-start.15
  93.8 0.0 collective-permute-done.18
  93.8 1.5 %collective-permute-start.16 = (bf16[2,512,128]{2,1,0:T(8,128)(2,1)S(1)}, bf16[2,512,128]{2,1,0:T(8,128)(2,1)S(1)}, u32[]{:S(2)}, u32[]{:S(2)}) collective-permute-start(bf16[2,512,128]{2,1,0:T(8,128)(2,1)S(1)} %get-tuple-element.18), channel_id=1, source_target_pairs={{64,0},{68,4},{72,8},{76,12},{80,16},{84,20},{88,24},{92,28},{96,3... | collective-permute-start | bytes 786440 | tf_op jit(solution)/shard_map/ppermute | solution.py:43
  95.2 0.0 collective-permute-done.19
  95.2 0.0 collective-permute-done.23
  95.2 0.1 add_convert_fusion.1
  95.3 0.7 fusion
  96.0 1.7 %collective-permute-done.14 = bf16[2,512,128]{2,1,0:T(8,128)(2,1)S(1)} collective-permute-done((bf16[2,512,128]{2,1,0:T(8,128)(2,1)S(1)}, bf16[2,512,128]{2,1,0:T(8,128)(2,1)S(1)}, u32[]{:S(2)}, u32[]{:S(2)}) %collective-permute-start.14) | collective-permute-done | bytes 262176 | tf_op jit(solution)/shard_map/ppermute | solution.py:43
  97.7 5.3 %collective-permute-done.15 = bf16[2,512,128]{2,1,0:T(8,128)(2,1)S(1)} collective-permute-done((bf16[2,512,128]{2,1,0:T(8,128)(2,1)S(1)}, bf16[2,512,128]{2,1,0:T(8,128)(2,1)S(1)}, u32[]{:S(2)}, u32[]{:S(2)}) %collective-permute-start.15) | collective-permute-done | bytes 262176 | tf_op jit(solution)/shard_map/ppermute | solution.py:43
  103.0 0.0 collective-permute-done.16
  103.0 0.1 add_convert_fusion
  103.1 0.9 copy.10
  (7 shorter events, 0.1 us)
Async XLA Ops:
  0.6 1.0 %copy-start.1 = (bf16[256,4,128]{2,1,0:T(4,128)(2,1)S(1)}, bf16[256,4,128]{2,1,0:T(4,128)(2,1)}, u32[]{:S(2)}) copy-start(bf16[256,4,128]{2,1,0:T(4,128)(2,1)} %param.8) | copy-start | bytes 786436
  1.7 2.5 %copy-start.2 = (bf16[256,1,128]{2,0,1:T(8,128)(2,1)S(1)}, bf16[256,1,128]{2,0,1:T(8,128)(2,1)}, u32[]{:S(2)}) copy-start(bf16[256,1,128]{2,0,1:T(8,128)(2,1)} %param.7) | copy-start | bytes 196612
  1.7 2.5 %copy-start.3 = (bf16[256,1,128]{2,0,1:T(8,128)(2,1)S(1)}, bf16[256,1,128]{2,0,1:T(8,128)(2,1)}, u32[]{:S(2)}) copy-start(bf16[256,1,128]{2,0,1:T(8,128)(2,1)} %param.6) | copy-start | bytes 196612
  1.8 13.9 %collective-permute-start.1 = (bf16[2,2,512,128]{3,2,1,0:T(8,128)(2,1)S(1)}, bf16[2,2,512,128]{3,2,1,0:T(8,128)(2,1)S(1)}, u32[]{:S(2)}, u32[]{:S(2)}) collective-permute-start(bf16[2,2,512,128]{3,2,1,0:T(8,128)(2,1)S(1)} %pad_maximum_fusion.refs_2_.refs_0_), channel_id=1, source_target_pairs={{96,0},{100,4},{104,8},{108,12},{112,16},{116,20},{120,24},{124,28... | collective-permute-start | bytes 1572872 | tf_op jit(solution)/shard_map/ppermute | solution.py:43
  3.4 15.2 %collective-permute-start = (bf16[2,2,512,128]{3,2,1,0:T(8,128)(2,1)S(1)}, bf16[2,2,512,128]{3,2,1,0:T(8,128)(2,1)S(1)}, u32[]{:S(2)}, u32[]{:S(2)}) collective-permute-start(bf16[2,2,512,128]{3,2,1,0:T(8,128)(2,1)S(1)} %pad_maximum_fusion.refs_2_.refs_0_), channel_id=1, source_target_pairs={{32,0},{36,4},{40,8},{44,12},{48,16},{52,20},{56,24},{60,28},{64,3... | collective-permute-start | bytes 1572872 | tf_op jit(solution)/shard_map/ppermute | solution.py:43
  4.2 15.9 %collective-permute-start.7 = (bf16[2,2,128,128]{3,2,1,0:T(8,128)(2,1)S(1)}, bf16[2,2,128,128]{3,2,1,0:T(8,128)(2,1)S(1)}, u32[]{:S(2)}, u32[]{:S(2)}) collective-permute-start(bf16[2,2,128,128]{3,2,1,0:T(8,128)(2,1)S(1)} %pad_maximum_fusion.1.refs_5_.refs_7_), channel_id=1, source_target_pairs={{16,0},{20,4},{24,8},{28,12},{0,16},{4,20},{8,24},{12,28},{48,32},... | collective-permute-start | bytes 393224 | tf_op jit(solution)/shard_map/ppermute | solution.py:43
  11.2 9.7 %collective-permute-start.6 = (bf16[2,2,128,128]{3,2,1,0:T(8,128)(2,1)S(1)}, bf16[2,2,128,128]{3,2,1,0:T(8,128)(2,1)S(1)}, u32[]{:S(2)}, u32[]{:S(2)}) collective-permute-start(bf16[2,2,128,128]{3,2,1,0:T(8,128)(2,1)S(1)} %pad_maximum_fusion.1.refs_5_.refs_7_), channel_id=1, source_target_pairs={{12,0},{0,4},{4,8},{8,12},{28,16},{16,20},{20,24},{24,28},{44,32},... | collective-permute-start | bytes 393224 | tf_op jit(solution)/shard_map/ppermute | solution.py:43
  12.8 8.1 %collective-permute-start.5 = (bf16[2,2,128,128]{3,2,1,0:T(8,128)(2,1)S(1)}, bf16[2,2,128,128]{3,2,1,0:T(8,128)(2,1)S(1)}, u32[]{:S(2)}, u32[]{:S(2)}) collective-permute-start(bf16[2,2,128,128]{3,2,1,0:T(8,128)(2,1)S(1)} %pad_maximum_fusion.1.refs_5_.refs_7_), channel_id=1, source_target_pairs={{8,0},{12,4},{0,8},{4,12},{24,16},{28,20},{16,24},{20,28},{40,32},... | collective-permute-start | bytes 393224 | tf_op jit(solution)/shard_map/ppermute | solution.py:43
  15.7 7.8 %collective-permute-start.4 = (bf16[2,2,128,128]{3,2,1,0:T(8,128)(2,1)S(1)}, bf16[2,2,128,128]{3,2,1,0:T(8,128)(2,1)S(1)}, u32[]{:S(2)}, u32[]{:S(2)}) collective-permute-start(bf16[2,2,128,128]{3,2,1,0:T(8,128)(2,1)S(1)} %pad_maximum_fusion.1.refs_5_.refs_7_), channel_id=1, source_target_pairs={{4,0},{8,4},{12,8},{0,12},{20,16},{24,20},{28,24},{16,28},{36,32},... | collective-permute-start | bytes 393224 | tf_op jit(solution)/shard_map/ppermute | solution.py:43
  18.6 12.1 %collective-permute-start.3 = (bf16[1,2,512,128]{3,2,1,0:T(8,128)(2,1)S(1)}, bf16[1,2,512,128]{3,2,1,0:T(8,128)(2,1)S(1)}, u32[]{:S(2)}, u32[]{:S(2)}) collective-permute-start(bf16[1,2,512,128]{3,2,1,0:T(8,128)(2,1)S(1)} %slice.17), channel_id=1, source_target_pairs={{96,0},{100,4},{104,8},{108,12},{112,16},{116,20},{120,24},{124,28... | collective-permute-start | bytes 786440 | tf_op jit(solution)/shard_map/ppermute | solution.py:43
  20.2 10.5 %collective-permute-start.2 = (bf16[1,2,512,128]{3,2,1,0:T(8,128)(2,1)S(1)}, bf16[1,2,512,128]{3,2,1,0:T(8,128)(2,1)S(1)}, u32[]{:S(2)}, u32[]{:S(2)}) collective-permute-start(bf16[1,2,512,128]{3,2,1,0:T(8,128)(2,1)S(1)} %slice.16), channel_id=1, source_target_pairs={{32,0},{36,4},{40,8},{44,12},{48,16},{52,20},{56,24},{60,28},{64,3... | collective-permute-start | bytes 786440 | tf_op jit(solution)/shard_map/ppermute | solution.py:43
  20.8 4.0 %copy-start = (s32[64]{0:T(128)S(1)}, s32[64]{0:T(128)}, u32[]{:S(2)}) copy-start(s32[64]{0:T(128)} %order_ref.1) | copy-start | bytes 772
  20.9 9.8 %collective-permute-start.10 = (bf16[2,2,128,128]{3,2,1,0:T(8,128)(2,1)S(1)}, bf16[2,2,128,128]{3,2,1,0:T(8,128)(2,1)S(1)}, u32[]{:S(2)}, u32[]{:S(2)}) collective-permute-start(bf16[2,2,128,128]{3,2,1,0:T(8,128)(2,1)S(1)} %collective-permute-done.7.refs_11_.refs_9_), channel_id=1, source_target_pairs={{12,0},{0,4},{4,8},{8,12},{28,16},{16,20},{20,24},{24,28},{44,32},... | collective-permute-start | bytes 393224 | tf_op jit(solution)/shard_map/ppermute | solution.py:43
  20.9 9.7 %collective-permute-start.9 = (bf16[2,2,128,128]{3,2,1,0:T(8,128)(2,1)S(1)}, bf16[2,2,128,128]{3,2,1,0:T(8,128)(2,1)S(1)}, u32[]{:S(2)}, u32[]{:S(2)}) collective-permute-start(bf16[2,2,128,128]{3,2,1,0:T(8,128)(2,1)S(1)} %collective-permute-done.7.refs_11_.refs_9_), channel_id=1, source_target_pairs={{8,0},{12,4},{0,8},{4,12},{24,16},{28,20},{16,24},{20,28},{40,32},... | collective-permute-start | bytes 393224 | tf_op jit(solution)/shard_map/ppermute | solution.py:43
  23.5 7.2 %collective-permute-start.8 = (bf16[2,2,128,128]{3,2,1,0:T(8,128)(2,1)S(1)}, bf16[2,2,128,128]{3,2,1,0:T(8,128)(2,1)S(1)}, u32[]{:S(2)}, u32[]{:S(2)}) collective-permute-start(bf16[2,2,128,128]{3,2,1,0:T(8,128)(2,1)S(1)} %collective-permute-done.7.refs_11_.refs_9_), channel_id=1, source_target_pairs={{4,0},{8,4},{12,8},{0,12},{20,16},{24,20},{28,24},{16,28},{36,32},... | collective-permute-start | bytes 393224 | tf_op jit(solution)/shard_map/ppermute | solution.py:43
  37.5 13.2 %collective-permute-start.13 = (f32[4,3,8,128]{3,2,1,0:T(8,128)S(1)}, f32[4,3,8,128]{3,2,1,0:T(8,128)S(1)}, u32[]{:S(2)}, u32[]{:S(2)}) collective-permute-start(f32[4,3,8,128]{3,2,1,0:T(8,128)S(1)} %row_stats.3.refs_13_), channel_id=1, source_target_pairs={{96,0},{100,4},{104,8},{108,12},{112,16},{116,20},{120,24},{124,28... | collective-permute-start | bytes 147464 | tf_op jit(solution)/shard_map/ppermute | solution.py:43
  48.4 5.6 %collective-permute-start.12 = (f32[4,3,8,128]{3,2,1,0:T(8,128)S(1)}, f32[4,3,8,128]{3,2,1,0:T(8,128)S(1)}, u32[]{:S(2)}, u32[]{:S(2)}) collective-permute-start(f32[4,3,8,128]{3,2,1,0:T(8,128)S(1)} %row_stats.3.refs_13_), channel_id=1, source_target_pairs={{64,0},{68,4},{72,8},{76,12},{80,16},{84,20},{88,24},{92,28},{96,3... | collective-permute-start | bytes 147464 | tf_op jit(solution)/shard_map/ppermute | solution.py:43
  48.4 5.6 %collective-permute-start.11 = (f32[4,3,8,128]{3,2,1,0:T(8,128)S(1)}, f32[4,3,8,128]{3,2,1,0:T(8,128)S(1)}, u32[]{:S(2)}, u32[]{:S(2)}) collective-permute-start(f32[4,3,8,128]{3,2,1,0:T(8,128)S(1)} %row_stats.3.refs_13_), channel_id=1, source_target_pairs={{32,0},{36,4},{40,8},{44,12},{48,16},{52,20},{56,24},{60,28},{64,3... | collective-permute-start | bytes 147464 | tf_op jit(solution)/shard_map/ppermute | solution.py:43
  70.2 8.6 %collective-permute-start.20 = (bf16[2,2,128,128]{3,2,1,0:T(8,128)(2,1)S(1)}, bf16[2,2,128,128]{3,2,1,0:T(8,128)(2,1)S(1)}, u32[]{:S(2)}, u32[]{:S(2)}) collective-permute-start(bf16[2,2,128,128]{3,2,1,0:T(8,128)(2,1)S(1)} %get-tuple-element.24), channel_id=1, source_target_pairs={{12,0},{0,4},{4,8},{8,12},{28,16},{16,20},{20,24},{24,28},{44,32},... | collective-permute-start | bytes 393224 | tf_op jit(solution)/shard_map/ppermute | solution.py:43
  70.3 8.8 %collective-permute-start.21 = (bf16[2,2,128,128]{3,2,1,0:T(8,128)(2,1)S(1)}, bf16[2,2,128,128]{3,2,1,0:T(8,128)(2,1)S(1)}, u32[]{:S(2)}, u32[]{:S(2)}) collective-permute-start(bf16[2,2,128,128]{3,2,1,0:T(8,128)(2,1)S(1)} %get-tuple-element.25), channel_id=1, source_target_pairs={{8,0},{12,4},{0,8},{4,12},{24,16},{28,20},{16,24},{20,28},{40,32},... | collective-permute-start | bytes 393224 | tf_op jit(solution)/shard_map/ppermute | solution.py:43
  71.5 7.9 %collective-permute-start.22 = (bf16[2,2,128,128]{3,2,1,0:T(8,128)(2,1)S(1)}, bf16[2,2,128,128]{3,2,1,0:T(8,128)(2,1)S(1)}, u32[]{:S(2)}, u32[]{:S(2)}) collective-permute-start(bf16[2,2,128,128]{3,2,1,0:T(8,128)(2,1)S(1)} %get-tuple-element.26), channel_id=1, source_target_pairs={{4,0},{8,4},{12,8},{0,12},{20,16},{24,20},{28,24},{16,28},{36,32},... | collective-permute-start | bytes 393224 | tf_op jit(solution)/shard_map/ppermute | solution.py:43
  73.5 20.3 %collective-permute-start.17 = (bf16[2,2,128,128]{3,2,1,0:T(8,128)(2,1)S(1)}, bf16[2,2,128,128]{3,2,1,0:T(8,128)(2,1)S(1)}, u32[]{:S(2)}, u32[]{:S(2)}) collective-permute-start(bf16[2,2,128,128]{3,2,1,0:T(8,128)(2,1)S(1)} %get-tuple-element.20), channel_id=1, source_target_pairs={{12,0},{0,4},{4,8},{8,12},{28,16},{16,20},{20,24},{24,28},{44,32},... | collective-permute-start | bytes 393224 | tf_op jit(solution)/shard_map/ppermute | solution.py:43
  74.4 19.4 %collective-permute-start.18 = (bf16[2,2,128,128]{3,2,1,0:T(8,128)(2,1)S(1)}, bf16[2,2,128,128]{3,2,1,0:T(8,128)(2,1)S(1)}, u32[]{:S(2)}, u32[]{:S(2)}) collective-permute-start(bf16[2,2,128,128]{3,2,1,0:T(8,128)(2,1)S(1)} %get-tuple-element.21), channel_id=1, source_target_pairs={{8,0},{12,4},{0,8},{4,12},{24,16},{28,20},{16,24},{20,28},{40,32},... | collective-permute-start | bytes 393224 | tf_op jit(solution)/shard_map/ppermute | solution.py:43
  78.8 16.4 %collective-permute-start.19 = (bf16[2,2,128,128]{3,2,1,0:T(8,128)(2,1)S(1)}, bf16[2,2,128,128]{3,2,1,0:T(8,128)(2,1)S(1)}, u32[]{:S(2)}, u32[]{:S(2)}) collective-permute-start(bf16[2,2,128,128]{3,2,1,0:T(8,128)(2,1)S(1)} %get-tuple-element.22), channel_id=1, source_target_pairs={{4,0},{8,4},{12,8},{0,12},{20,16},{24,20},{28,24},{16,28},{36,32},... | collective-permute-start | bytes 393224 | tf_op jit(solution)/shard_map/ppermute | solution.py:43
  79.5 15.7 %collective-permute-start.23 = (bf16[2,2,128,128]{3,2,1,0:T(8,128)(2,1)S(1)}, bf16[2,2,128,128]{3,2,1,0:T(8,128)(2,1)S(1)}, u32[]{:S(2)}, u32[]{:S(2)}) collective-permute-start(bf16[2,2,128,128]{3,2,1,0:T(8,128)(2,1)S(1)} %add_convert_fusion.2), channel_id=1, source_target_pairs={{16,0},{20,4},{24,8},{28,12},{0,16},{4,20},{8,24},{12,28},{48,32},... | collective-permute-start | bytes 393224 | tf_op jit(solution)/shard_map/ppermute | solution.py:43
  90.9 6.8 %collective-permute-start.14 = (bf16[2,512,128]{2,1,0:T(8,128)(2,1)S(1)}, bf16[2,512,128]{2,1,0:T(8,128)(2,1)S(1)}, u32[]{:S(2)}, u32[]{:S(2)}) collective-permute-start(bf16[2,512,128]{2,1,0:T(8,128)(2,1)S(1)} %get-tuple-element.16), channel_id=1, source_target_pairs={{96,0},{100,4},{104,8},{108,12},{112,16},{116,20},{120,24},{124,28... | collective-permute-start | bytes 786440 | tf_op jit(solution)/shard_map/ppermute | solution.py:43
  93.8 9.2 %collective-permute-start.15 = (bf16[2,512,128]{2,1,0:T(8,128)(2,1)S(1)}, bf16[2,512,128]{2,1,0:T(8,128)(2,1)S(1)}, u32[]{:S(2)}, u32[]{:S(2)}) collective-permute-start(bf16[2,512,128]{2,1,0:T(8,128)(2,1)S(1)} %get-tuple-element.17), channel_id=1, source_target_pairs={{32,0},{36,4},{40,8},{44,12},{48,16},{52,20},{56,24},{60,28},{64,3... | collective-permute-start | bytes 786440 | tf_op jit(solution)/shard_map/ppermute | solution.py:43
  93.8 9.2 %collective-permute-start.16 = (bf16[2,512,128]{2,1,0:T(8,128)(2,1)S(1)}, bf16[2,512,128]{2,1,0:T(8,128)(2,1)S(1)}, u32[]{:S(2)}, u32[]{:S(2)}) collective-permute-start(bf16[2,512,128]{2,1,0:T(8,128)(2,1)S(1)} %get-tuple-element.18), channel_id=1, source_target_pairs={{64,0},{68,4},{72,8},{76,12},{80,16},{84,20},{88,24},{92,28},{96,3... | collective-permute-start | bytes 786440 | tf_op jit(solution)/shard_map/ppermute | solution.py:43
where the time goes:
time: 104 us
  starting transfers between devices  58.2 us (56%)
  Pallas kernels  28.8 us (28%)
  waiting for transfers between devices  13 us (12%)
  local copies, waits for them, and re-layouts  2.69 us (3%)
    ppermute x24, starting transfers between devices, fetch(): return lax.ppermute(a, 'ctx', shift(**d))  58.2 us
    pallas_call x1, Pallas kernels, grads_call(): pl.pallas_call(grads_kernel, out_shape=[jax.ShapeDtypeStruct((LOCAL, ROWS...  16.2 us
    ppermute x24, waiting for transfers between devices, fetch(): return lax.ppermute(a, 'ctx', shift(**d))  13 us
    pallas_call x2, Pallas kernels, stats_call(): pl.pallas_call(lambda *refs: stats_kernel(rows, keys, *refs), out_shape=j...  12.6 us
  transfers between devices with their start and end apart: 24, of which 5 were waited for; matrix products, arithmetic and copies ran while one was open for 1% of the time, Pallas kernels for 6%

commit v1 on v0

--- a/solution.py
+++ b/solution.py
@@ -397,9 +397,10 @@
     own = add([own[0]] + [fetch(own[t], dy=-t) for t in range(1, Y)] + [other]).astype(jnp.bfloat16)
     key_gradient = own[0].reshape(LOCAL * SPAN, 1, D)
     value_gradient = own[1].reshape(LOCAL * SPAN, 1, D)
-    total = add([dq[0]] + [fetch(dq[i], dx=-s) for i, s in enumerate(LINE) if i > 0])
+    parts = [dq[0]] + [fetch(dq[i], dx=-s) for i, s in enumerate(LINE) if i > 0]
     query_grad = (
-        total.astype(jnp.bfloat16)
+        add(parts)
+        .astype(jnp.bfloat16)
         .reshape(LOCAL, HEADS, SPAN, D)
         .transpose(0, 2, 1, 3)
         .reshape(LOCAL * SPAN, HEADS, D)

time: 104 us -> 104 us (level)
  no operation moved by 1% of the time
where the time goes in v1:
time: 104 us
  starting transfers between devices  58.2 us (56%)
  Pallas kernels  28.8 us (28%)
  waiting for transfers between devices  13 us (12%)
  local copies, waits for them, and re-layouts  2.69 us (3%)
    ppermute x24, starting transfers between devices, fetch(): return lax.ppermute(a, 'ctx', shift(**d))  58.2 us
    pallas_call x1, Pallas kernels, grads_call(): pl.pallas_call(grads_kernel, out_shape=[jax.ShapeDtypeStruct((LOCAL, ROWS...  16.2 us
    ppermute x24, waiting for transfers between devices, fetch(): return lax.ppermute(a, 'ctx', shift(**d))  13 us
    pallas_call x2, Pallas kernels, stats_call(): pl.pallas_call(lambda *refs: stats_kernel(rows, keys, *refs), out_shape=j...  12.6 us
  transfers between devices with their start and end apart: 24, of which 5 were waited for; matrix products, arithmetic and copies ran while one was open for 1% of the time, Pallas kernels for 6%

profile of v1, /device:TPU:2, one launch (start us, length us, event | category | flops | bytes accessed | tf_op | source)
XLA Modules:
  0.0 104.0 jit_solution(8192751265451658744)
XLA Ops:
  0.6 0.0 copy-start.1
  0.6 1.0 copy.8
  1.7 0.0 copy-done.1
  1.7 0.0 copy-start.2
  1.7 0.0 copy-start.3
  1.8 0.1 pad_maximum_fusion.refs_2_.refs_0_
  1.8 1.6 %collective-permute-start.1 = (bf16[2,2,512,128]{3,2,1,0:T(8,128)(2,1)S(1)}, bf16[2,2,512,128]{3,2,1,0:T(8,128)(2,1)S(1)}, u32[]{:S(2)}, u32[]{:S(2)}) collective-permute-start(bf16[2,2,512,128]{3,2,1,0:T(8,128)(2,1)S(1)} %pad_maximum_fusion.refs_2_.refs_0_), channel_id=1, source_target_pairs={{96,0},{100,4},{104,8},{108,12},{112,16},{116,20},{120,24},{124,28... | collective-permute-start | bytes 1572872 | tf_op jit(solution)/shard_map/ppermute | solution.py:43
  3.4 0.8 collective-permute-start
  4.2 0.0 copy-done.2
  4.2 7.0 %collective-permute-start.7 = (bf16[2,2,128,128]{3,2,1,0:T(8,128)(2,1)S(1)}, bf16[2,2,128,128]{3,2,1,0:T(8,128)(2,1)S(1)}, u32[]{:S(2)}, u32[]{:S(2)}) collective-permute-start(bf16[2,2,128,128]{3,2,1,0:T(8,128)(2,1)S(1)} %pad_maximum_fusion.1.refs_5_.refs_7_), channel_id=1, source_target_pairs={{16,0},{20,4},{24,8},{28,12},{0,16},{4,20},{8,24},{12,28},{48,32},... | collective-permute-start | bytes 393224 | tf_op jit(solution)/shard_map/ppermute | solution.py:43
  11.2 1.6 %collective-permute-start.6 = (bf16[2,2,128,128]{3,2,1,0:T(8,128)(2,1)S(1)}, bf16[2,2,128,128]{3,2,1,0:T(8,128)(2,1)S(1)}, u32[]{:S(2)}, u32[]{:S(2)}) collective-permute-start(bf16[2,2,128,128]{3,2,1,0:T(8,128)(2,1)S(1)} %pad_maximum_fusion.1.refs_5_.refs_7_), channel_id=1, source_target_pairs={{12,0},{0,4},{4,8},{8,12},{28,16},{16,20},{20,24},{24,28},{44,32},... | collective-permute-start | bytes 393224 | tf_op jit(solution)/shard_map/ppermute | solution.py:43
  12.8 2.9 %collective-permute-start.5 = (bf16[2,2,128,128]{3,2,1,0:T(8,128)(2,1)S(1)}, bf16[2,2,128,128]{3,2,1,0:T(8,128)(2,1)S(1)}, u32[]{:S(2)}, u32[]{:S(2)}) collective-permute-start(bf16[2,2,128,128]{3,2,1,0:T(8,128)(2,1)S(1)} %pad_maximum_fusion.1.refs_5_.refs_7_), channel_id=1, source_target_pairs={{8,0},{12,4},{0,8},{4,12},{24,16},{28,20},{16,24},{20,28},{40,32},... | collective-permute-start | bytes 393224 | tf_op jit(solution)/shard_map/ppermute | solution.py:43
  15.7 0.0 collective-permute-done.1.refs_4_.refs_2_
  15.7 2.9 %collective-permute-start.4 = (bf16[2,2,128,128]{3,2,1,0:T(8,128)(2,1)S(1)}, bf16[2,2,128,128]{3,2,1,0:T(8,128)(2,1)S(1)}, u32[]{:S(2)}, u32[]{:S(2)}) collective-permute-start(bf16[2,2,128,128]{3,2,1,0:T(8,128)(2,1)S(1)} %pad_maximum_fusion.1.refs_5_.refs_7_), channel_id=1, source_target_pairs={{4,0},{8,4},{12,8},{0,12},{20,16},{24,20},{28,24},{16,28},{36,32},... | collective-permute-start | bytes 393224 | tf_op jit(solution)/shard_map/ppermute | solution.py:43
  18.6 0.0 collective-permute-done.refs_3_.refs_1_
  18.6 1.6 %collective-permute-start.3 = (bf16[1,2,512,128]{3,2,1,0:T(8,128)(2,1)S(1)}, bf16[1,2,512,128]{3,2,1,0:T(8,128)(2,1)S(1)}, u32[]{:S(2)}, u32[]{:S(2)}) collective-permute-start(bf16[1,2,512,128]{3,2,1,0:T(8,128)(2,1)S(1)} %slice.17), channel_id=1, source_target_pairs={{96,0},{100,4},{104,8},{108,12},{112,16},{116,20},{120,24},{124,28... | collective-permute-start | bytes 786440 | tf_op jit(solution)/shard_map/ppermute | solution.py:43
  20.2 0.0 collective-permute-done.7.refs_11_.refs_9_
  20.2 0.6 collective-permute-start.2
  20.8 0.1 pad_add_fusion.refs_1_.pos_ref
  20.9 0.0 collective-permute-done.6.refs_8_.refs_10_
  20.9 0.0 collective-permute-start.10
  20.9 0.0 collective-permute-done.5.refs_7_.refs_9_
  20.9 2.5 %collective-permute-start.9 = (bf16[2,2,128,128]{3,2,1,0:T(8,128)(2,1)S(1)}, bf16[2,2,128,128]{3,2,1,0:T(8,128)(2,1)S(1)}, u32[]{:S(2)}, u32[]{:S(2)}) collective-permute-start(bf16[2,2,128,128]{3,2,1,0:T(8,128)(2,1)S(1)} %collective-permute-done.7.refs_11_.refs_9_), channel_id=1, source_target_pairs={{8,0},{12,4},{0,8},{4,12},{24,16},{28,20},{16,24},{20,28},{40,32},... | collective-permute-start | bytes 393224 | tf_op jit(solution)/shard_map/ppermute | solution.py:43
  23.5 0.0 collective-permute-done.4.refs_6_.refs_8_
  23.5 1.3 %collective-permute-start.8 = (bf16[2,2,128,128]{3,2,1,0:T(8,128)(2,1)S(1)}, bf16[2,2,128,128]{3,2,1,0:T(8,128)(2,1)S(1)}, u32[]{:S(2)}, u32[]{:S(2)}) collective-permute-start(bf16[2,2,128,128]{3,2,1,0:T(8,128)(2,1)S(1)} %collective-permute-done.7.refs_11_.refs_9_), channel_id=1, source_target_pairs={{4,0},{8,4},{12,8},{0,12},{20,16},{24,20},{28,24},{16,28},{36,32},... | collective-permute-start | bytes 393224 | tf_op jit(solution)/shard_map/ppermute | solution.py:43
  24.8 5.8 %row_stats.2.refs_15_ = f32[3,3,8,128]{3,2,1,0:T(8,128)S(1)} custom-call(s32[64]{0:T(128)S(1)} %copy-done, s32[3]{0:T(128)S(1)} %pad_add_fusion.refs_1_.pos_ref, bf16[2,2,512,128]{3,2,1,0:T(8,128)(2,1)S(1)} %pad_maximum_fusion.refs_2_.refs_0_, bf16[2,2,512,128]{3,2,1,0:T(8,128)(2,1)S(1)} %collective-permute-done.refs_3_.refs_1_, ...), custom_call_target="tpu_custom_call" | custom-call | flops 1610612736 | bytes 2097152 | tf_op jit(solution)/shard_map/row_stats/pallas_call | solution.py:333
  30.7 0.0 collective-permute-done.10.refs_14_.refs_12_
  30.7 0.0 collective-permute-done.9.refs_13_.refs_11_
  30.7 0.0 collective-permute-done.8.refs_12_.refs_10_
  30.7 0.0 collective-permute-done.3.refs_6_.refs_4_
  30.7 0.0 collective-permute-done.2.refs_5_.refs_3_
  30.7 6.8 %row_stats.3.refs_13_ = f32[4,3,8,128]{3,2,1,0:T(8,128)S(1)} custom-call(s32[64]{0:T(128)S(1)} %copy-done, s32[3]{0:T(128)S(1)} %pad_add_fusion.refs_1_.pos_ref, bf16[2,2,512,128]{3,2,1,0:T(8,128)(2,1)S(1)} %pad_maximum_fusion.refs_2_.refs_0_, bf16[2,2,512,128]{3,2,1,0:T(8,128)(2,1)S(1)} %collective-permute-done.refs_3_.refs_1_, ...), custom_call_target="tpu_custom_call" | custom-call | flops 4294967296 | bytes 3145728 | tf_op jit(solution)/shard_map/row_stats/pallas_call | solution.py:333
  37.5 10.8 %collective-permute-start.13 = (f32[4,3,8,128]{3,2,1,0:T(8,128)S(1)}, f32[4,3,8,128]{3,2,1,0:T(8,128)S(1)}, u32[]{:S(2)}, u32[]{:S(2)}) collective-permute-start(f32[4,3,8,128]{3,2,1,0:T(8,128)S(1)} %row_stats.3.refs_13_), channel_id=1, source_target_pairs={{96,0},{100,4},{104,8},{108,12},{112,16},{116,20},{120,24},{124,28... | collective-permute-start | bytes 147464 | tf_op jit(solution)/shard_map/ppermute | solution.py:43
  48.4 0.0 collective-permute-start.12
  48.4 2.3 %collective-permute-start.11 = (f32[4,3,8,128]{3,2,1,0:T(8,128)S(1)}, f32[4,3,8,128]{3,2,1,0:T(8,128)S(1)}, u32[]{:S(2)}, u32[]{:S(2)}) collective-permute-start(f32[4,3,8,128]{3,2,1,0:T(8,128)S(1)} %row_stats.3.refs_13_), channel_id=1, source_target_pairs={{32,0},{36,4},{40,8},{44,12},{48,16},{52,20},{56,24},{60,28},{64,3... | collective-permute-start | bytes 147464 | tf_op jit(solution)/shard_map/ppermute | solution.py:43
  50.7 0.0 collective-permute-done.13.refs_16_
  50.7 3.2 %collective-permute-done.12.refs_15_ = f32[4,3,8,128]{3,2,1,0:T(8,128)S(1)} collective-permute-done((f32[4,3,8,128]{3,2,1,0:T(8,128)S(1)}, f32[4,3,8,128]{3,2,1,0:T(8,128)S(1)}, u32[]{:S(2)}, u32[]{:S(2)}) %collective-permute-start.12) | collective-permute-done | bytes 49184 | tf_op jit(solution)/shard_map/ppermute | solution.py:43
  53.9 0.0 collective-permute-done.11.refs_14_
  54.0 16.2 %gradients.1 = (bf16[2,512,128]{2,1,0:T(8,128)(2,1)S(1)}, bf16[2,512,128]{2,1,0:T(8,128)(2,1)S(1)}, bf16[2,512,128]{2,1,0:T(8,128)(2,1)S(1)}, bf16[2,512,128]{2,...) custom-call(s32[64]{0:T(128)S(1)} %copy-done, ...), custom_call_target="tpu_custom_call" | custom-call | flops 10737418240 | bytes 3145728 | tf_op jit(solution)/shard_map/gradients/pallas_call | solution.py:347
  70.2 0.1 collective-permute-start.20
  70.3 1.2 %collective-permute-start.21 = (bf16[2,2,128,128]{3,2,1,0:T(8,128)(2,1)S(1)}, bf16[2,2,128,128]{3,2,1,0:T(8,128)(2,1)S(1)}, u32[]{:S(2)}, u32[]{:S(2)}) collective-permute-start(bf16[2,2,128,128]{3,2,1,0:T(8,128)(2,1)S(1)} %get-tuple-element.25), channel_id=1, source_target_pairs={{8,0},{12,4},{0,8},{4,12},{24,16},{28,20},{16,24},{20,28},{40,32},... | collective-permute-start | bytes 393224 | tf_op jit(solution)/shard_map/ppermute | solution.py:43
  71.5 2.0 %collective-permute-start.22 = (bf16[2,2,128,128]{3,2,1,0:T(8,128)(2,1)S(1)}, bf16[2,2,128,128]{3,2,1,0:T(8,128)(2,1)S(1)}, u32[]{:S(2)}, u32[]{:S(2)}) collective-permute-start(bf16[2,2,128,128]{3,2,1,0:T(8,128)(2,1)S(1)} %get-tuple-element.26), channel_id=1, source_target_pairs={{4,0},{8,4},{12,8},{0,12},{20,16},{24,20},{28,24},{16,28},{36,32},... | collective-permute-start | bytes 393224 | tf_op jit(solution)/shard_map/ppermute | solution.py:43
  73.5 0.9 collective-permute-start.17
  74.4 2.1 %collective-permute-start.18 = (bf16[2,2,128,128]{3,2,1,0:T(8,128)(2,1)S(1)}, bf16[2,2,128,128]{3,2,1,0:T(8,128)(2,1)S(1)}, u32[]{:S(2)}, u32[]{:S(2)}) collective-permute-start(bf16[2,2,128,128]{3,2,1,0:T(8,128)(2,1)S(1)} %get-tuple-element.21), channel_id=1, source_target_pairs={{8,0},{12,4},{0,8},{4,12},{24,16},{28,20},{16,24},{20,28},{40,32},... | collective-permute-start | bytes 393224 | tf_op jit(solution)/shard_map/ppermute | solution.py:43
  76.4 2.4 %collective-permute-done.20 = bf16[2,2,128,128]{3,2,1,0:T(8,128)(2,1)S(1)} collective-permute-done((bf16[2,2,128,128]{3,2,1,0:T(8,128)(2,1)S(1)}, bf16[2,2,128,128]{3,2,1,0:T(8,128)(2,1)S(1)}, u32[]{:S(2)}, u32[]{:S(2)}) %collective-permute-start.20) | collective-permute-done | bytes 131104 | tf_op jit(solution)/shard_map/ppermute | solution.py:43
  78.8 0.2 collective-permute-start.19
  79.1 0.0 collective-permute-done.21
  79.1 0.4 collective-permute-done.22
  79.5 0.1 add_convert_fusion.2
  79.5 11.4 %collective-permute-start.23 = (bf16[2,2,128,128]{3,2,1,0:T(8,128)(2,1)S(1)}, bf16[2,2,128,128]{3,2,1,0:T(8,128)(2,1)S(1)}, u32[]{:S(2)}, u32[]{:S(2)}) collective-permute-start(bf16[2,2,128,128]{3,2,1,0:T(8,128)(2,1)S(1)} %add_convert_fusion.2), channel_id=1, source_target_pairs={{16,0},{20,4},{24,8},{28,12},{0,16},{4,20},{8,24},{12,28},{48,32},... | collective-permute-start | bytes 393224 | tf_op jit(solution)/shard_map/ppermute | solution.py:43
  90.9 2.9 %collective-permute-start.14 = (bf16[2,512,128]{2,1,0:T(8,128)(2,1)S(1)}, bf16[2,512,128]{2,1,0:T(8,128)(2,1)S(1)}, u32[]{:S(2)}, u32[]{:S(2)}) collective-permute-start(bf16[2,512,128]{2,1,0:T(8,128)(2,1)S(1)} %get-tuple-element.16), channel_id=1, source_target_pairs={{96,0},{100,4},{104,8},{108,12},{112,16},{116,20},{120,24},{124,28... | collective-permute-start | bytes 786440 | tf_op jit(solution)/shard_map/ppermute | solution.py:43
  93.8 0.0 collective-permute-done.17
  93.8 0.0 collective-permute-start.15
  93.8 0.0 collective-permute-done.18
  93.8 1.5 %collective-permute-start.16 = (bf16[2,512,128]{2,1,0:T(8,128)(2,1)S(1)}, bf16[2,512,128]{2,1,0:T(8,128)(2,1)S(1)}, u32[]{:S(2)}, u32[]{:S(2)}) collective-permute-start(bf16[2,512,128]{2,1,0:T(8,128)(2,1)S(1)} %get-tuple-element.18), channel_id=1, source_target_pairs={{64,0},{68,4},{72,8},{76,12},{80,16},{84,20},{88,24},{92,28},{96,3... | collective-permute-start | bytes 786440 | tf_op jit(solution)/shard_map/ppermute | solution.py:43
  95.2 0.0 collective-permute-done.19
  95.2 0.0 collective-permute-done.23
  95.2 0.1 add_convert_fusion.1
  95.3 0.7 fusion
  96.0 1.7 %collective-permute-done.14 = bf16[2,512,128]{2,1,0:T(8,128)(2,1)S(1)} collective-permute-done((bf16[2,512,128]{2,1,0:T(8,128)(2,1)S(1)}, bf16[2,512,128]{2,1,0:T(8,128)(2,1)S(1)}, u32[]{:S(2)}, u32[]{:S(2)}) %collective-permute-start.14) | collective-permute-done | bytes 262176 | tf_op jit(solution)/shard_map/ppermute | solution.py:43
  97.7 5.3 %collective-permute-done.15 = bf16[2,512,128]{2,1,0:T(8,128)(2,1)S(1)} collective-permute-done((bf16[2,512,128]{2,1,0:T(8,128)(2,1)S(1)}, bf16[2,512,128]{2,1,0:T(8,128)(2,1)S(1)}, u32[]{:S(2)}, u32[]{:S(2)}) %collective-permute-start.15) | collective-permute-done | bytes 262176 | tf_op jit(solution)/shard_map/ppermute | solution.py:43
  103.0 0.0 collective-permute-done.16
  103.0 0.1 add_convert_fusion
  103.1 0.9 copy.10
  (7 shorter events, 0.1 us)
Async XLA Ops:
  0.6 1.0 %copy-start.1 = (bf16[256,4,128]{2,1,0:T(4,128)(2,1)S(1)}, bf16[256,4,128]{2,1,0:T(4,128)(2,1)}, u32[]{:S(2)}) copy-start(bf16[256,4,128]{2,1,0:T(4,128)(2,1)} %param.8) | copy-start | bytes 786436
  1.7 2.5 %copy-start.2 = (bf16[256,1,128]{2,0,1:T(8,128)(2,1)S(1)}, bf16[256,1,128]{2,0,1:T(8,128)(2,1)}, u32[]{:S(2)}) copy-start(bf16[256,1,128]{2,0,1:T(8,128)(2,1)} %param.7) | copy-start | bytes 196612
  1.7 2.5 %copy-start.3 = (bf16[256,1,128]{2,0,1:T(8,128)(2,1)S(1)}, bf16[256,1,128]{2,0,1:T(8,128)(2,1)}, u32[]{:S(2)}) copy-start(bf16[256,1,128]{2,0,1:T(8,128)(2,1)} %param.6) | copy-start | bytes 196612
  1.8 13.9 %collective-permute-start.1 = (bf16[2,2,512,128]{3,2,1,0:T(8,128)(2,1)S(1)}, bf16[2,2,512,128]{3,2,1,0:T(8,128)(2,1)S(1)}, u32[]{:S(2)}, u32[]{:S(2)}) collective-permute-start(bf16[2,2,512,128]{3,2,1,0:T(8,128)(2,1)S(1)} %pad_maximum_fusion.refs_2_.refs_0_), channel_id=1, source_target_pairs={{96,0},{100,4},{104,8},{108,12},{112,16},{116,20},{120,24},{124,28... | collective-permute-start | bytes 1572872 | tf_op jit(solution)/shard_map/ppermute | solution.py:43
  3.4 15.2 %collective-permute-start = (bf16[2,2,512,128]{3,2,1,0:T(8,128)(2,1)S(1)}, bf16[2,2,512,128]{3,2,1,0:T(8,128)(2,1)S(1)}, u32[]{:S(2)}, u32[]{:S(2)}) collective-permute-start(bf16[2,2,512,128]{3,2,1,0:T(8,128)(2,1)S(1)} %pad_maximum_fusion.refs_2_.refs_0_), channel_id=1, source_target_pairs={{32,0},{36,4},{40,8},{44,12},{48,16},{52,20},{56,24},{60,28},{64,3... | collective-permute-start | bytes 1572872 | tf_op jit(solution)/shard_map/ppermute | solution.py:43
  4.2 15.9 %collective-permute-start.7 = (bf16[2,2,128,128]{3,2,1,0:T(8,128)(2,1)S(1)}, bf16[2,2,128,128]{3,2,1,0:T(8,128)(2,1)S(1)}, u32[]{:S(2)}, u32[]{:S(2)}) collective-permute-start(bf16[2,2,128,128]{3,2,1,0:T(8,128)(2,1)S(1)} %pad_maximum_fusion.1.refs_5_.refs_7_), channel_id=1, source_target_pairs={{16,0},{20,4},{24,8},{28,12},{0,16},{4,20},{8,24},{12,28},{48,32},... | collective-permute-start | bytes 393224 | tf_op jit(solution)/shard_map/ppermute | solution.py:43
  11.2 9.7 %collective-permute-start.6 = (bf16[2,2,128,128]{3,2,1,0:T(8,128)(2,1)S(1)}, bf16[2,2,128,128]{3,2,1,0:T(8,128)(2,1)S(1)}, u32[]{:S(2)}, u32[]{:S(2)}) collective-permute-start(bf16[2,2,128,128]{3,2,1,0:T(8,128)(2,1)S(1)} %pad_maximum_fusion.1.refs_5_.refs_7_), channel_id=1, source_target_pairs={{12,0},{0,4},{4,8},{8,12},{28,16},{16,20},{20,24},{24,28},{44,32},... | collective-permute-start | bytes 393224 | tf_op jit(solution)/shard_map/ppermute | solution.py:43
  12.8 8.1 %collective-permute-start.5 = (bf16[2,2,128,128]{3,2,1,0:T(8,128)(2,1)S(1)}, bf16[2,2,128,128]{3,2,1,0:T(8,128)(2,1)S(1)}, u32[]{:S(2)}, u32[]{:S(2)}) collective-permute-start(bf16[2,2,128,128]{3,2,1,0:T(8,128)(2,1)S(1)} %pad_maximum_fusion.1.refs_5_.refs_7_), channel_id=1, source_target_pairs={{8,0},{12,4},{0,8},{4,12},{24,16},{28,20},{16,24},{20,28},{40,32},... | collective-permute-start | bytes 393224 | tf_op jit(solution)/shard_map/ppermute | solution.py:43
  15.7 7.8 %collective-permute-start.4 = (bf16[2,2,128,128]{3,2,1,0:T(8,128)(2,1)S(1)}, bf16[2,2,128,128]{3,2,1,0:T(8,128)(2,1)S(1)}, u32[]{:S(2)}, u32[]{:S(2)}) collective-permute-start(bf16[2,2,128,128]{3,2,1,0:T(8,128)(2,1)S(1)} %pad_maximum_fusion.1.refs_5_.refs_7_), channel_id=1, source_target_pairs={{4,0},{8,4},{12,8},{0,12},{20,16},{24,20},{28,24},{16,28},{36,32},... | collective-permute-start | bytes 393224 | tf_op jit(solution)/shard_map/ppermute | solution.py:43
  18.6 12.1 %collective-permute-start.3 = (bf16[1,2,512,128]{3,2,1,0:T(8,128)(2,1)S(1)}, bf16[1,2,512,128]{3,2,1,0:T(8,128)(2,1)S(1)}, u32[]{:S(2)}, u32[]{:S(2)}) collective-permute-start(bf16[1,2,512,128]{3,2,1,0:T(8,128)(2,1)S(1)} %slice.17), channel_id=1, source_target_pairs={{96,0},{100,4},{104,8},{108,12},{112,16},{116,20},{120,24},{124,28... | collective-permute-start | bytes 786440 | tf_op jit(solution)/shard_map/ppermute | solution.py:43
  20.2 10.5 %collective-permute-start.2 = (bf16[1,2,512,128]{3,2,1,0:T(8,128)(2,1)S(1)}, bf16[1,2,512,128]{3,2,1,0:T(8,128)(2,1)S(1)}, u32[]{:S(2)}, u32[]{:S(2)}) collective-permute-start(bf16[1,2,512,128]{3,2,1,0:T(8,128)(2,1)S(1)} %slice.16), channel_id=1, source_target_pairs={{32,0},{36,4},{40,8},{44,12},{48,16},{52,20},{56,24},{60,28},{64,3... | collective-permute-start | bytes 786440 | tf_op jit(solution)/shard_map/ppermute | solution.py:43
  20.8 4.0 %copy-start = (s32[64]{0:T(128)S(1)}, s32[64]{0:T(128)}, u32[]{:S(2)}) copy-start(s32[64]{0:T(128)} %order_ref.1) | copy-start | bytes 772
  20.9 9.8 %collective-permute-start.10 = (bf16[2,2,128,128]{3,2,1,0:T(8,128)(2,1)S(1)}, bf16[2,2,128,128]{3,2,1,0:T(8,128)(2,1)S(1)}, u32[]{:S(2)}, u32[]{:S(2)}) collective-permute-start(bf16[2,2,128,128]{3,2,1,0:T(8,128)(2,1)S(1)} %collective-permute-done.7.refs_11_.refs_9_), channel_id=1, source_target_pairs={{12,0},{0,4},{4,8},{8,12},{28,16},{16,20},{20,24},{24,28},{44,32},... | collective-permute-start | bytes 393224 | tf_op jit(solution)/shard_map/ppermute | solution.py:43
  20.9 9.7 %collective-permute-start.9 = (bf16[2,2,128,128]{3,2,1,0:T(8,128)(2,1)S(1)}, bf16[2,2,128,128]{3,2,1,0:T(8,128)(2,1)S(1)}, u32[]{:S(2)}, u32[]{:S(2)}) collective-permute-start(bf16[2,2,128,128]{3,2,1,0:T(8,128)(2,1)S(1)} %collective-permute-done.7.refs_11_.refs_9_), channel_id=1, source_target_pairs={{8,0},{12,4},{0,8},{4,12},{24,16},{28,20},{16,24},{20,28},{40,32},... | collective-permute-start | bytes 393224 | tf_op jit(solution)/shard_map/ppermute | solution.py:43
  23.5 7.2 %collective-permute-start.8 = (bf16[2,2,128,128]{3,2,1,0:T(8,128)(2,1)S(1)}, bf16[2,2,128,128]{3,2,1,0:T(8,128)(2,1)S(1)}, u32[]{:S(2)}, u32[]{:S(2)}) collective-permute-start(bf16[2,2,128,128]{3,2,1,0:T(8,128)(2,1)S(1)} %collective-permute-done.7.refs_11_.refs_9_), channel_id=1, source_target_pairs={{4,0},{8,4},{12,8},{0,12},{20,16},{24,20},{28,24},{16,28},{36,32},... | collective-permute-start | bytes 393224 | tf_op jit(solution)/shard_map/ppermute | solution.py:43
  37.5 13.2 %collective-permute-start.13 = (f32[4,3,8,128]{3,2,1,0:T(8,128)S(1)}, f32[4,3,8,128]{3,2,1,0:T(8,128)S(1)}, u32[]{:S(2)}, u32[]{:S(2)}) collective-permute-start(f32[4,3,8,128]{3,2,1,0:T(8,128)S(1)} %row_stats.3.refs_13_), channel_id=1, source_target_pairs={{96,0},{100,4},{104,8},{108,12},{112,16},{116,20},{120,24},{124,28... | collective-permute-start | bytes 147464 | tf_op jit(solution)/shard_map/ppermute | solution.py:43
  48.4 5.6 %collective-permute-start.12 = (f32[4,3,8,128]{3,2,1,0:T(8,128)S(1)}, f32[4,3,8,128]{3,2,1,0:T(8,128)S(1)}, u32[]{:S(2)}, u32[]{:S(2)}) collective-permute-start(f32[4,3,8,128]{3,2,1,0:T(8,128)S(1)} %row_stats.3.refs_13_), channel_id=1, source_target_pairs={{64,0},{68,4},{72,8},{76,12},{80,16},{84,20},{88,24},{92,28},{96,3... | collective-permute-start | bytes 147464 | tf_op jit(solution)/shard_map/ppermute | solution.py:43
  48.4 5.6 %collective-permute-start.11 = (f32[4,3,8,128]{3,2,1,0:T(8,128)S(1)}, f32[4,3,8,128]{3,2,1,0:T(8,128)S(1)}, u32[]{:S(2)}, u32[]{:S(2)}) collective-permute-start(f32[4,3,8,128]{3,2,1,0:T(8,128)S(1)} %row_stats.3.refs_13_), channel_id=1, source_target_pairs={{32,0},{36,4},{40,8},{44,12},{48,16},{52,20},{56,24},{60,28},{64,3... | collective-permute-start | bytes 147464 | tf_op jit(solution)/shard_map/ppermute | solution.py:43
  70.2 8.6 %collective-permute-start.20 = (bf16[2,2,128,128]{3,2,1,0:T(8,128)(2,1)S(1)}, bf16[2,2,128,128]{3,2,1,0:T(8,128)(2,1)S(1)}, u32[]{:S(2)}, u32[]{:S(2)}) collective-permute-start(bf16[2,2,128,128]{3,2,1,0:T(8,128)(2,1)S(1)} %get-tuple-element.24), channel_id=1, source_target_pairs={{12,0},{0,4},{4,8},{8,12},{28,16},{16,20},{20,24},{24,28},{44,32},... | collective-permute-start | bytes 393224 | tf_op jit(solution)/shard_map/ppermute | solution.py:43
  70.3 8.8 %collective-permute-start.21 = (bf16[2,2,128,128]{3,2,1,0:T(8,128)(2,1)S(1)}, bf16[2,2,128,128]{3,2,1,0:T(8,128)(2,1)S(1)}, u32[]{:S(2)}, u32[]{:S(2)}) collective-permute-start(bf16[2,2,128,128]{3,2,1,0:T(8,128)(2,1)S(1)} %get-tuple-element.25), channel_id=1, source_target_pairs={{8,0},{12,4},{0,8},{4,12},{24,16},{28,20},{16,24},{20,28},{40,32},... | collective-permute-start | bytes 393224 | tf_op jit(solution)/shard_map/ppermute | solution.py:43
  71.5 7.9 %collective-permute-start.22 = (bf16[2,2,128,128]{3,2,1,0:T(8,128)(2,1)S(1)}, bf16[2,2,128,128]{3,2,1,0:T(8,128)(2,1)S(1)}, u32[]{:S(2)}, u32[]{:S(2)}) collective-permute-start(bf16[2,2,128,128]{3,2,1,0:T(8,128)(2,1)S(1)} %get-tuple-element.26), channel_id=1, source_target_pairs={{4,0},{8,4},{12,8},{0,12},{20,16},{24,20},{28,24},{16,28},{36,32},... | collective-permute-start | bytes 393224 | tf_op jit(solution)/shard_map/ppermute | solution.py:43
  73.5 20.3 %collective-permute-start.17 = (bf16[2,2,128,128]{3,2,1,0:T(8,128)(2,1)S(1)}, bf16[2,2,128,128]{3,2,1,0:T(8,128)(2,1)S(1)}, u32[]{:S(2)}, u32[]{:S(2)}) collective-permute-start(bf16[2,2,128,128]{3,2,1,0:T(8,128)(2,1)S(1)} %get-tuple-element.20), channel_id=1, source_target_pairs={{12,0},{0,4},{4,8},{8,12},{28,16},{16,20},{20,24},{24,28},{44,32},... | collective-permute-start | bytes 393224 | tf_op jit(solution)/shard_map/ppermute | solution.py:43
  74.4 19.4 %collective-permute-start.18 = (bf16[2,2,128,128]{3,2,1,0:T(8,128)(2,1)S(1)}, bf16[2,2,128,128]{3,2,1,0:T(8,128)(2,1)S(1)}, u32[]{:S(2)}, u32[]{:S(2)}) collective-permute-start(bf16[2,2,128,128]{3,2,1,0:T(8,128)(2,1)S(1)} %get-tuple-element.21), channel_id=1, source_target_pairs={{8,0},{12,4},{0,8},{4,12},{24,16},{28,20},{16,24},{20,28},{40,32},... | collective-permute-start | bytes 393224 | tf_op jit(solution)/shard_map/ppermute | solution.py:43
  78.8 16.4 %collective-permute-start.19 = (bf16[2,2,128,128]{3,2,1,0:T(8,128)(2,1)S(1)}, bf16[2,2,128,128]{3,2,1,0:T(8,128)(2,1)S(1)}, u32[]{:S(2)}, u32[]{:S(2)}) collective-permute-start(bf16[2,2,128,128]{3,2,1,0:T(8,128)(2,1)S(1)} %get-tuple-element.22), channel_id=1, source_target_pairs={{4,0},{8,4},{12,8},{0,12},{20,16},{24,20},{28,24},{16,28},{36,32},... | collective-permute-start | bytes 393224 | tf_op jit(solution)/shard_map/ppermute | solution.py:43
  79.5 15.7 %collective-permute-start.23 = (bf16[2,2,128,128]{3,2,1,0:T(8,128)(2,1)S(1)}, bf16[2,2,128,128]{3,2,1,0:T(8,128)(2,1)S(1)}, u32[]{:S(2)}, u32[]{:S(2)}) collective-permute-start(bf16[2,2,128,128]{3,2,1,0:T(8,128)(2,1)S(1)} %add_convert_fusion.2), channel_id=1, source_target_pairs={{16,0},{20,4},{24,8},{28,12},{0,16},{4,20},{8,24},{12,28},{48,32},... | collective-permute-start | bytes 393224 | tf_op jit(solution)/shard_map/ppermute | solution.py:43
  90.9 6.8 %collective-permute-start.14 = (bf16[2,512,128]{2,1,0:T(8,128)(2,1)S(1)}, bf16[2,512,128]{2,1,0:T(8,128)(2,1)S(1)}, u32[]{:S(2)}, u32[]{:S(2)}) collective-permute-start(bf16[2,512,128]{2,1,0:T(8,128)(2,1)S(1)} %get-tuple-element.16), channel_id=1, source_target_pairs={{96,0},{100,4},{104,8},{108,12},{112,16},{116,20},{120,24},{124,28... | collective-permute-start | bytes 786440 | tf_op jit(solution)/shard_map/ppermute | solution.py:43
  93.8 9.2 %collective-permute-start.15 = (bf16[2,512,128]{2,1,0:T(8,128)(2,1)S(1)}, bf16[2,512,128]{2,1,0:T(8,128)(2,1)S(1)}, u32[]{:S(2)}, u32[]{:S(2)}) collective-permute-start(bf16[2,512,128]{2,1,0:T(8,128)(2,1)S(1)} %get-tuple-element.17), channel_id=1, source_target_pairs={{32,0},{36,4},{40,8},{44,12},{48,16},{52,20},{56,24},{60,28},{64,3... | collective-permute-start | bytes 786440 | tf_op jit(solution)/shard_map/ppermute | solution.py:43
  93.8 9.2 %collective-permute-start.16 = (bf16[2,512,128]{2,1,0:T(8,128)(2,1)S(1)}, bf16[2,512,128]{2,1,0:T(8,128)(2,1)S(1)}, u32[]{:S(2)}, u32[]{:S(2)}) collective-permute-start(bf16[2,512,128]{2,1,0:T(8,128)(2,1)S(1)} %get-tuple-element.18), channel_id=1, source_target_pairs={{64,0},{68,4},{72,8},{76,12},{80,16},{84,20},{88,24},{92,28},{96,3... | collective-permute-start | bytes 786440 | tf_op jit(solution)/shard_map/ppermute | solution.py:43
